TPU v7x, 32 devices: a whole 2x2x4 slice. The times are simulated.
32 devices in a mesh: seq: 16 (over z, y, core), dp: 2 (over x).
Axes of the slice: x: 2, y: 2, z: 4, core: 2. Of those that a mesh axis runs over, the one named last changes fastest.
Arguments:
- q_student: bfloat16 [2, 8192, 1536], P('dp', 'seq'), may hold values from -8 to 8
- kv_student: bfloat16 [2, 128, 3072], P('dp', 'seq'), may hold values from -8 to 8
- q_target: bfloat16 [2, 8192, 1536], P('dp', 'seq'), may hold values from -8 to 8
- kv_target: bfloat16 [2, 128, 3072], P('dp', 'seq'), may hold values from -8 to 8
Outputs:
- student_out: bfloat16 [2, 8192, 1536], P('dp', 'seq')
- target_out: bfloat16 [2, 8192, 1536], P('dp', 'seq')
- distill_loss: float32 [], replicated
All inputs are finite; a program needn't handle non-finite values.
Results may differ from a plain program's by a relative error of at most 0.004.
Values may be sent and summed in bfloat16 or wider, within the bound.
A program may use at most 128 MiB of HBM per device.

v0:
```python
import jax
import jax.numpy as jnp
from jax import lax
from jax.sharding import PartitionSpec as P

HEADS = 12
HD = 128


def absorb(query3, carried, incoming):
    running_max, running_sum, running_out = carried
    block_pairs = incoming[0]
    key_rows = block_pairs.shape[0]
    feature_width = HEADS * HD
    key_block = block_pairs[:, :feature_width].reshape(key_rows, HEADS, HD)
    value_block = block_pairs[:, feature_width:].reshape(key_rows, HEADS, HD)
    scores = jnp.einsum("qhd,khd->hqk", query3, key_block, preferred_element_type=jnp.float32) * (
        1.0 / HD**0.5
    )
    new_max = jnp.maximum(running_max, jnp.max(scores, axis=-1))
    shrink = jnp.exp(running_max - new_max)
    exponent = jnp.exp(scores - new_max[:, :, None])
    running_sum = jnp.sum(exponent, axis=-1)
    running_out = jnp.einsum(
        "hqk,khd->hqd",
        exponent.astype(jnp.bfloat16),
        value_block,
        preferred_element_type=jnp.float32,
    )
    return (new_max, running_sum, running_out)


def normalize(carried, query_rows):
    running_max, running_sum, running_out = carried
    mixed_rows = running_out / running_sum[:, :, None]
    return jnp.transpose(mixed_rows, (1, 0, 2)).reshape(query_rows, HEADS * HD)


def body(q_student, kv_student, q_target, kv_target):
    query_rows = q_student.shape[1]
    student_query = q_student[0].reshape(query_rows, HEADS, HD)
    target_query = q_target[0].reshape(query_rows, HEADS, HD)
    initial = (
        jnp.full((HEADS, query_rows), -1e30, jnp.float32),
        jnp.zeros((HEADS, query_rows), jnp.float32),
        jnp.zeros((HEADS, query_rows, HD), jnp.float32),
    )
    student_all = lax.all_gather(kv_student, "seq", axis=1, tiled=True)
    target_all = lax.all_gather(kv_target, "seq", axis=1, tiled=True)
    student_carry = absorb(student_query, initial, student_all)
    target_carry = absorb(target_query, initial, target_all)
    student_rows = normalize(student_carry, query_rows)
    target_rows = normalize(target_carry, query_rows)
    seq_count = lax.axis_size("seq")
    all_tokens = query_rows * seq_count
    position = (lax.axis_index("seq") * query_rows + jnp.arange(query_rows)).astype(jnp.float32)
    weight = 1.0 + 2.0 * position / float(max(all_tokens - 1, 1))
    gap_rows = student_rows - target_rows
    local_term = jnp.sum(weight[:, None] * gap_rows * gap_rows) / float(all_tokens * HEADS * HD)
    clip_term = lax.psum(local_term, "seq")
    distill_loss = lax.psum(clip_term, "dp")
    return (
        student_rows[None].astype(jnp.bfloat16),
        target_rows[None].astype(jnp.bfloat16),
        distill_loss,
    )


def solution(mesh):
    return jax.shard_map(
        body,
        mesh=mesh,
        in_specs=(
            P("dp", "seq", None),
            P("dp", "seq", None),
            P("dp", "seq", None),
            P("dp", "seq", None),
        ),
        out_specs=(P("dp", "seq", None), P("dp", "seq", None), P()),
        check_vma=False,
    )
```

profile of v0, /device:TPU:0, one launch (start us, length us, event | category | flops | bytes accessed | tf_op | source)
XLA Modules:
  0.0 106.9 jit_solution(2824079883674600560)
XLA Ops:
  0.6 0.0 copy-start
  0.6 25.9 %all_gather.7 = bf16[1,128,3072]{2,1,0:T(8,128)(2,1)S(1)} all-gather(bf16[1,8,3072]{2,1,0:T(8,128)(2,1)} %param.7), channel_id=1, replica_groups=mesh['seq'=16,'dp'=2] {'seq'}, dimensions={1}, use_global_device_ids=true | all-gather | bytes 835584 | tf_op jit(solution)/shard_map/all_gather | solution.py:49
  26.5 0.4 copy.33
  26.9 0.8 fusion.13
  27.7 0.0 copy-done
  27.7 0.7 copy.32
  28.4 0.0 copy-start.4
  28.4 0.6 multiply_reduce_fusion
  29.1 0.6 fusion.3
  29.6 0.0 copy-done.4
  29.6 0.0 copy-start.6
  29.6 2.5 %bitcast_divide_fusion = f32[512,12,128]{0,2,1:T(8,128)} fusion(bf16[128,12,128]{0,2,1:T(8,128)(2,1)S(1)} %bitcast.31, f32[12,512,128]{1,2,0:T(8,128)S(1)} %get-tuple-element.22, f32[512,12]{0,1:T(8,128)S(1)} %bitcast.33, f32[12,512]{1,0:T(8,128)S(1)} %broadcast_maximum_fusion), kind=kOutput, calls=%fused_computation.2 | convolution fusion | flops 204472320 | bytes 6733824 | tf_op jit(solution)/shard_map/hqk,khd->hqd/dot_general | solution.py:24
  32.2 0.0 copy-done.6
  32.2 0.0 copy-start.1
  32.2 19.7 %all_gather.6 = bf16[1,128,3072]{2,1,0:T(8,128)(2,1)S(1)} all-gather(bf16[1,8,3072]{2,1,0:T(8,128)(2,1)S(1)} %copy-done.6), channel_id=1, replica_groups=mesh['seq'=16,'dp'=2] {'seq'}, dimensions={1}, use_global_device_ids=true | all-gather | bytes 835584 | tf_op jit(solution)/shard_map/all_gather | solution.py:48
  51.9 0.4 copy.28
  52.3 0.8 fusion.14
  53.1 0.0 copy-done.1
  53.1 1.6 %copy.27 = bf16[1,512,1536]{1,2,0:T(8,128)(2,1)} copy(bf16[1,512,1536]{2,1,0:T(8,128)(2,1)S(1)} %copy-done.1) | data formatting | bytes 3145728 | tf_op args[0]
  54.7 2.0 %multiply_reduce_fusion.1 = (f32[12,512]{1,0:T(8,128)S(1)}, f32[12,512,128]{1,2,0:T(8,128)S(1)}) fusion(bf16[512,12,128]{0,2,1:T(8,128)(2,1)} %bitcast.23, bf16[128,12,128]{0,2,1:T(8,128)(2,1)S(1)} %bitcast.29), kind=kOutput, calls=%fused_computation.7 | convolution fusion | flops 202893312 | bytes 5136384 | tf_op jit(solution)/shard_map/qhd,khd->hqk/dot_general | solution.py:17
  56.7 0.0 copy-start.3
  56.7 0.0 copy-start.5
  56.7 0.6 copy-done.5
  57.3 1.2 %fusion.1 = f32[12,512]{1,0:T(8,128)} fusion(f32[12,512,128]{1,2,0:T(8,128)S(1)} %get-tuple-element.20, f32[12,512]{1,0:T(8,128)S(1)} %broadcast_maximum_fusion.1), kind=kLoop, calls=%fused_computation.8 | loop fusion | flops 2353152 | bytes 3194880 | tf_op jit(solution)/shard_map/reduce_sum | solution.py:23
  58.5 0.0 copy-done.3
  58.5 6.3 %fusion = (f32[]{:T(128)}, bf16[512,12,128]{0,2,1:T(8,128)(2,1)}, bf16[512,12,128]{0,2,1:T(8,128)(2,1)}) fusion(f32[512,12,128]{0,2,1:T(8,128)} %bitcast_divide_fusion, f32[512]{0:T(512)S(1)} %multiply_add_fusion, f32[512,12]{0,1:T(8,128)} %bitcast.32, bf16[128,12,128]{0,2,1:T(8,128)(2,1)S(1)} %bitcast.30, f32[12,512,128]{1,2,0:T(8,128)S(1)} %get-tuple-element.20, ...), kind=kOutput, calls=%fused_computation.1 | convolution fusion | flops 209190912 | bytes 9881604 | tf_op jit(solution)/shard_map/hqk,khd->hqd/dot_general | solution.py:24
  64.8 0.0 copy-start.2
  64.8 2.7 %copy.37 = bf16[1,512,1536]{2,1,0:T(8,128)(2,1)} copy(bf16[1,512,1536]{1,2,0:T(8,128)(2,1)} %bitcast.27) | data formatting | bytes 3145728
  67.5 0.0 copy-done.2
  67.5 1.6 %copy.38 = bf16[1,512,1536]{2,1,0:T(8,128)(2,1)} copy(bf16[1,512,1536]{1,2,0:T(8,128)(2,1)S(1)} %bitcast.26) | data formatting | bytes 3145728
  69.7 31.7 %psum.14 = f32[]{:T(128)} all-reduce(f32[]{:T(128)S(6)} %div.39), channel_id=1, replica_groups=mesh['seq'=16,'dp'=2] {'seq'}, use_global_device_ids=true, to_apply=%region_5.0 | all-reduce | flops 1 | bytes 8 | tf_op jit(solution)/shard_map/psum | solution.py:60
  101.4 5.5 %psum.15 = f32[]{:T(128)} all-reduce(f32[]{:T(128)} %psum.14), channel_id=1, replica_groups=mesh['seq'=16,'dp'=2] {'dp'}, use_global_device_ids=true, to_apply=%region_6.0 | all-reduce | flops 1 | bytes 8 | tf_op jit(solution)/shard_map/psum | solution.py:61
  (3 shorter events, 0.0 us)
Async XLA Ops:
  0.6 27.1 %copy-start = (bf16[1,512,1536]{2,1,0:T(8,128)(2,1)S(1)}, bf16[1,512,1536]{2,1,0:T(8,128)(2,1)}, u32[]{:S(2)}) copy-start(bf16[1,512,1536]{2,1,0:T(8,128)(2,1)} %param.6) | copy-start | bytes 4718596
  28.4 1.2 %copy-start.4 = (bf16[128,1536]{0,1:T(8,128)(2,1)S(1)}, bf16[128,1536]{0,1:T(8,128)(2,1)}, u32[]{:S(2)}) copy-start(bf16[128,1536]{0,1:T(8,128)(2,1)} %get-tuple-element.16) | copy-start | bytes 1179652
  29.6 2.5 %copy-start.6 = (bf16[1,8,3072]{2,1,0:T(8,128)(2,1)S(1)}, bf16[1,8,3072]{2,1,0:T(8,128)(2,1)}, u32[]{:S(2)}) copy-start(bf16[1,8,3072]{2,1,0:T(8,128)(2,1)} %param.5) | copy-start | bytes 147460
  32.2 20.9 %copy-start.1 = (bf16[1,512,1536]{2,1,0:T(8,128)(2,1)S(1)}, bf16[1,512,1536]{2,1,0:T(8,128)(2,1)}, u32[]{:S(2)}) copy-start(bf16[1,512,1536]{2,1,0:T(8,128)(2,1)} %param.4) | copy-start | bytes 4718596
  56.7 1.8 %copy-start.3 = (bf16[128,1536]{0,1:T(8,128)(2,1)S(1)}, bf16[128,1536]{0,1:T(8,128)(2,1)}, u32[]{:S(2)}) copy-start(bf16[128,1536]{0,1:T(8,128)(2,1)} %get-tuple-element.18) | copy-start | bytes 1179652
  56.7 0.6 copy-start.5
  64.8 2.7 %copy-start.2 = (bf16[512,12,128]{0,2,1:T(8,128)(2,1)S(1)}, bf16[512,12,128]{0,2,1:T(8,128)(2,1)}, u32[]{:S(2)}) copy-start(bf16[512,12,128]{0,2,1:T(8,128)(2,1)} %get-tuple-element.13) | copy-start | bytes 4718596
where the time goes:
time: 107 us
  blocking collectives  82.8 us (77%)
  matrix products  11.5 us (11%)
  local copies, waits for them, and re-layouts  9.49 us (9%)
  other arithmetic  1.75 us (2%)
  between operations  1.39 us (1%)
    psum x1, blocking collectives, body(): clip_term = lax.psum(local_term, 'seq')  31.7 us
    all_gather x1, blocking collectives, body(): target_all = lax.all_gather(kv_target, 'seq', axis=1, tiled=True)  25.9 us
    all_gather x1, blocking collectives, body(): student_all = lax.all_gather(kv_student, 'seq', axis=1, tiled=True)  19.7 us
    dot_general x2, matrix products, absorb(): jnp.einsum('hqk,khd->hqd', exponent.astype(jnp.bfloat16), value_block, pr...  8.79 us
    unnamed x18, local copies, waits for them, and re-layouts  7.15 us
    psum x1, blocking collectives, body(): distill_loss = lax.psum(clip_term, 'dp')  5.54 us
    dot_general x2, matrix products, absorb(): jnp.einsum('qhd,khd->hqk', query3, key_block, preferred_element_type=jnp....  2.66 us

commit v1 on v0

--- a/solution.py
+++ b/solution.py
@@ -45,8 +45,11 @@
         jnp.zeros((HEADS, query_rows), jnp.float32),
         jnp.zeros((HEADS, query_rows, HD), jnp.float32),
     )
-    student_all = lax.all_gather(kv_student, "seq", axis=1, tiled=True)
-    target_all = lax.all_gather(kv_target, "seq", axis=1, tiled=True)
+    student_all, target_all = jnp.split(
+        lax.all_gather(jnp.concatenate([kv_student, kv_target], axis=0), "seq", axis=1, tiled=True),
+        [kv_student.shape[0]],
+        axis=0,
+    )
     student_carry = absorb(student_query, initial, student_all)
     target_carry = absorb(target_query, initial, target_all)
     student_rows = normalize(student_carry, query_rows)

time: 107 us -> 123 us (1.15)
  blocking collectives: 82.8 us -> 37.4 us
  waiting for transfers between devices: 0 us -> 40.1 us
  between operations: 1.39 us -> 14.8 us
  local copies, waits for them, and re-layouts: 9.49 us -> 20.6 us
  matrix products: 11.5 us -> 6.74 us
    all_gather x2 -> x0, blocking collectives: 45.6 us -> none  [the longest x1 25.9 us: body(): target_all = lax.all_gather(kv_target, 'seq', axis=1, tiled=True)]
    all_gather x0 -> x1, waiting for transfers between devices: none -> 40.1 us  [body(): lax.all_gather(jnp.concatenate([kv_student, kv_target], axis=0), 'seq', a...]
    dot_general x2, matrix products: 8.79 us -> 2.64 us  [absorb(): jnp.einsum('hqk,khd->hqd', exponent.astype(jnp.bfloat16), value_block, pr...]
    unnamed x18 -> x10, local copies, waits for them, and re-layouts: 7.15 us -> 13.3 us
    split x0 -> x1, local copies, waits for them, and re-layouts: none -> 5.34 us  [body(): jnp.split(lax.all_gather(jnp.concatenate([kv_student, kv_target], axis=0)...]
    dot_general x2, matrix products: 2.66 us -> 4.1 us  [absorb(): jnp.einsum('qhd,khd->hqk', query3, key_block, preferred_element_type=jnp....]
  transfers between devices with their start and end apart: 0 -> 1, of which waited for: 0 -> 1; matrix products, arithmetic and copies ran while one was open for 0% -> 3% of each run, Pallas kernels for 0% -> 0%
where the time goes in v1:
time: 123 us; the launch traced here: 122 us
  waiting for transfers between devices  40.1 us (33%)
  blocking collectives  37.4 us (30%)
  local copies, waits for them, and re-layouts  20.6 us (17%)
  between operations  14.8 us (12%)
  matrix products  6.74 us (5%)
  other arithmetic  2.7 us (2%)
    all_gather x1, waiting for transfers between devices, body(): lax.all_gather(jnp.concatenate([kv_student, kv_target], axis=0), 'seq', a...  40.1 us
    psum x1, blocking collectives, body(): clip_term = lax.psum(local_term, 'seq')  31.8 us
    unnamed x10, local copies, waits for them, and re-layouts  13.3 us
    psum x1, blocking collectives, body(): distill_loss = lax.psum(clip_term, 'dp')  5.54 us
    split x1, local copies, waits for them, and re-layouts, body(): jnp.split(lax.all_gather(jnp.concatenate([kv_student, kv_target], axis=0)...  5.34 us
    dot_general x2, matrix products, absorb(): jnp.einsum('qhd,khd->hqk', query3, key_block, preferred_element_type=jnp....  4.1 us
    dot_general x2, matrix products, absorb(): jnp.einsum('hqk,khd->hqd', exponent.astype(jnp.bfloat16), value_block, pr...  2.64 us
  transfers between devices with their start and end apart: 1, of which 1 were waited for; matrix products, arithmetic and copies ran while one was open for 3% of the time, Pallas kernels for 0%

profile of v1, /device:TPU:0, one launch (start us, length us, event | category | flops | bytes accessed | tf_op | source)
XLA Modules:
  0.0 122.3 jit_solution(5500302214122509078)
XLA Ops:
  7.2 0.0 copy-start
  7.2 0.0 all-gather.2.cloned.1.call-start
  7.2 0.9 pad_maximum_fusion
  8.2 0.7 copy.27
  8.9 0.0 all-gather.2.cloned.1.call-update
  8.9 2.6 %copy.34 = bf16[1,512,1536]{1,2,0:T(8,128)(2,1)} copy(bf16[1,512,1536]{2,1,0:T(8,128)(2,1)} %param.6) | data formatting | bytes 3145728 | tf_op args[2]
  11.5 0.0 copy-done
  11.5 1.6 %copy.29 = bf16[1,512,1536]{1,2,0:T(8,128)(2,1)} copy(bf16[1,512,1536]{2,1,0:T(8,128)(2,1)S(1)} %copy-done) | data formatting | bytes 3145728 | tf_op args[0]
  13.1 40.1 %all-gather.2.cloned.1.call-done = bf16[2,128,3072]{2,0,1:T(2,128)(2,1)} async-done(((bf16[2,8,3072]{2,0,1:T(2,128)(2,1)}), bf16[2,128,3072]{2,0,1:T(2,128)(2,1)}) %all-gather.2.cloned.1.call-update) | async-done | bytes 1572880 | tf_op jit(solution)/shard_map/all_gather | solution.py:49
  53.2 5.3 %fusion.15 = (bf16[1,128,3072]{2,0,1:T(2,128)(2,1)S(1)}, bf16[1,128,3072]{2,0,1:T(2,128)(2,1)}) fusion(bf16[2,128,3072]{2,0,1:T(2,128)(2,1)} %all-gather.2.cloned.1.call-done), kind=kLoop, calls=%fused_computation.24 | loop fusion | bytes 3145728 | tf_op jit(solution)/shard_map/split | solution.py:48
  58.5 1.8 %copy.47 = bf16[1,128,3072]{1,2,0:T(8,128)(2,1)S(1)} copy(bf16[1,128,3072]{2,0,1:T(2,128)(2,1)S(1)} %get-tuple-element.15) | data formatting | bytes 1572864
  60.3 0.1 fusion.16
  60.4 2.1 %bitcast_reduce_fusion = (f32[12,512]{1,0:T(8,128)S(1)}, f32[12,128,512]{2,1,0:T(8,128)S(1)}) fusion(bf16[128,12,128]{0,2,1:T(8,128)(2,1)S(1)} %bitcast.50, bf16[512,12,128]{0,2,1:T(8,128)(2,1)} %bitcast.45), kind=kOutput, calls=%fused_computation.4 | convolution fusion | flops 202893312 | bytes 5136384 | tf_op jit(solution)/shard_map/qhd,khd->hqk/dot_general | solution.py:17
  62.4 0.6 broadcast_maximum_fusion
  63.0 4.2 %copy.46 = bf16[1,128,3072]{1,2,0:T(8,128)(2,1)} copy(bf16[1,128,3072]{2,0,1:T(2,128)(2,1)} %get-tuple-element.16) | data formatting | bytes 1572864
  67.2 0.0 copy-start.1
  67.2 1.2 fusion.17
  68.4 2.0 %bitcast_reduce_fusion.1 = (f32[12,512]{1,0:T(8,128)S(1)}, f32[12,128,512]{2,1,0:T(8,128)S(1)}) fusion(bf16[128,12,128]{0,2,1:T(8,128)(2,1)S(1)} %bitcast.51, bf16[512,12,128]{0,2,1:T(8,128)(2,1)} %bitcast.44), kind=kOutput, calls=%fused_computation.8 | convolution fusion | flops 202893312 | bytes 5136384 | tf_op jit(solution)/shard_map/qhd,khd->hqk/dot_general | solution.py:17
  70.5 0.0 copy-done.1
  70.5 0.6 fusion.5
  71.0 0.9 bitcast_divide_fusion
  71.9 0.6 fusion.3
  72.5 1.8 %fusion = (f32[]{:T(128)}, bf16[512,12,128]{0,2,1:T(8,128)(2,1)S(1)}, bf16[512,12,128]{0,2,1:T(8,128)(2,1)S(1)}) fusion(f32[512,12,128]{0,2,1:T(8,128)S(1)} %bitcast_divide_fusion, f32[512]{0:T(512)S(1)} %multiply_add_fusion, f32[512,12]{0,1:T(8,128)S(1)} %bitcast.54, bf16[128,12,128]{0,2,1:T(8,128)(2,1)S(1)} %bitcast.53, ...), kind=kOutput, calls=%fused_computation.1 | convolution fusion | flops 209190912 | bytes 9881604 | tf_op jit(solution)/shard_map/hqk,khd->hqd/dot_general | solution.py:24
  74.9 1.6 %copy.38 = bf16[1,512,1536]{2,1,0:T(8,128)(2,1)} copy(bf16[1,512,1536]{1,2,0:T(8,128)(2,1)S(1)} %bitcast.49) | data formatting | bytes 3145728
  76.5 31.8 %psum.14 = f32[]{:T(128)} all-reduce(f32[]{:T(128)S(6)} %div.39), channel_id=1, replica_groups=mesh['seq'=16,'dp'=2] {'seq'}, use_global_device_ids=true, to_apply=%region_5.0 | all-reduce | flops 1 | bytes 8 | tf_op jit(solution)/shard_map/psum | solution.py:63
  108.3 1.6 %copy.39 = bf16[1,512,1536]{2,1,0:T(8,128)(2,1)} copy(bf16[1,512,1536]{1,2,0:T(8,128)(2,1)S(1)} %bitcast.48) | data formatting | bytes 3145728
  109.9 5.5 %psum.15 = f32[]{:T(128)} all-reduce(f32[]{:T(128)} %psum.14), channel_id=1, replica_groups=mesh['seq'=16,'dp'=2] {'dp'}, use_global_device_ids=true, to_apply=%region_6.0 | all-reduce | flops 1 | bytes 8 | tf_op jit(solution)/shard_map/psum | solution.py:64
  (2 shorter events, 0.0 us)
Async XLA Ops:
  7.2 4.4 %copy-start = (bf16[1,512,1536]{2,1,0:T(8,128)(2,1)S(1)}, bf16[1,512,1536]{2,1,0:T(8,128)(2,1)}, u32[]{:S(2)}) copy-start(bf16[1,512,1536]{2,1,0:T(8,128)(2,1)} %param.4) | copy-start | bytes 4718596
  7.2 46.0 %all-gather.2.cloned.1.call-start = ((), (), s32[]{:S(2)}) async-start(), calls=%async_computation | async-start | bytes 1671168 | tf_op jit(solution)/shard_map/all_gather | solution.py:49
  67.2 3.2 %copy-start.1 = (f32[12,512]{1,0:T(8,128)S(1)}, f32[12,512]{1,0:T(8,128)}, u32[]{:S(2)}) copy-start(f32[12,512]{1,0:T(8,128)} %broadcast_maximum_fusion) | copy-start | bytes 73732
Sparse Core Ops, SparseCore 0:
  10.8 42.3 all-gather.1
